TPU v7x, 256 devices: a whole 4x4x8 slice. The times are simulated.
256 devices in a mesh: section: 4 (over x), tensor: 16 (over z, core), dp: 4 (over y).
Axes of the slice: x: 4, y: 4, z: 8, core: 2. Of those that a mesh axis runs over, the one named last changes fastest.
Arguments:
- hidden_in: bfloat16 [128, 4096], P('dp', 'tensor'), may hold values from -6 to 6
- norm_gain: float32 [4, 4096], P('section'), may hold values from 0.25 to 1.75
- gate_weight: bfloat16 [4, 4096, 8192], P('section', 'dp', 'tensor'), may hold values from -0.09375 to 0.09375
- up_weight: bfloat16 [4, 4096, 8192], P('section', 'dp', 'tensor'), may hold values from -0.09375 to 0.09375
- down_weight: bfloat16 [4, 4096, 8192], P('section', 'dp', 'tensor'), may hold values from -0.0625 to 0.0625
- lengths: int32 [16], P('dp'), may hold values from 3 to 8
Outputs:
- rdm: float32 [4, 16, 16], P('section', 'dp')
Inputs may be any that keep to these rules, and one draw needn't show every extreme that they name: `lengths`: the number of leading valid token rows of each sentence.
All inputs are finite; a program needn't handle non-finite values.
Results may differ from a plain program's by a relative error of at most 0.0012.
Values may be sent and summed in bfloat16 or wider, within the bound.
A program may use at most 128 MiB of HBM per device.

v0:
```python
import jax
import jax.numpy as jnp
from jax import lax
from jax.sharding import PartitionSpec as P

D = 4096
LEN = 8
MICRO = 2
SENT_DEV = 4
SENT_MB = 2
MB_TOK = 16


RMS_EPS = 1e-05
UNIT_FLOOR = 0.1
CONTRACT_LAST = (((1,), (1,)), ((), ()))


def side_by_side(arrays, axis, dim, along):
    ends, at = ([], 0)
    for a in arrays[:-1]:
        at += a.shape[along]
        ends.append(at)
    both = jnp.concatenate(arrays, axis=along)
    return tuple(jnp.split(lax.all_gather(both, axis, axis=dim, tiled=True), ends, axis=along))


def in_order(pieces, dim):
    pieces = jnp.moveaxis(pieces, 0, dim)
    shape = pieces.shape
    return pieces.reshape(*shape[:dim], shape[dim] * shape[dim + 1], *shape[dim + 2 :])


def sent_to_all(array, axis):
    copies = jnp.broadcast_to(array, (lax.axis_size(axis), *array.shape))
    return lax.all_to_all(copies, axis, split_axis=0, concat_axis=0, tiled=True)


def gathered_copies(array, axis, dim):
    return in_order(sent_to_all(array, axis), dim)


def in_blocks(array, dim, peers):
    shape = array.shape
    pieces = array.reshape(*shape[:dim], peers, shape[dim] // peers, *shape[dim + 1 :])
    return jnp.moveaxis(pieces, dim, 0)


def sent_and_summed(array, axis, dim):
    peers = lax.axis_size(axis)
    pieces = lax.all_to_all(in_blocks(array, dim, peers), axis, 0, 0, tiled=True)
    return jnp.sum(pieces.astype(jnp.float32), axis=0)


def passed_along(array, axis, by):
    peers = lax.axis_size(axis)
    pairs = [(i, i + by) for i in range(peers) if 0 <= i + by < peers]
    return lax.ppermute(array, axis, pairs)


def pool_rows(values, sentence_len):
    shaped = values.astype(jnp.float32).reshape(SENT_MB, LEN, values.shape[1])
    positions = jnp.arange(LEN, dtype=jnp.int32)
    weights = (positions[None, :] < sentence_len[:, None]).astype(jnp.float32)
    return jnp.sum(shaped * weights[:, :, None], axis=1) / sentence_len.astype(jnp.float32)[:, None]


def per_device(hidden_in, norm_gain, gate_weight, up_weight, down_weight, lengths):
    section_index = lax.axis_index("section")
    tick_count = MICRO + lax.axis_size("section") - 1
    gate_full, up_full, down_full = side_by_side(
        (gate_weight[0], up_weight[0], down_weight[0]), "dp", 0, 1
    )
    gain_full = norm_gain[0]
    columns = D // lax.axis_size("tensor")
    tensor_index = lax.axis_index("tensor")

    def plan(step_index):
        micro_index = step_index - section_index
        active = jnp.logical_and(micro_index >= 0, micro_index < MICRO)
        clipped = jnp.clip(micro_index, 0, MICRO - 1)
        return (active, clipped)

    def store_unit(pooled_units, unit_rows, active, clipped):
        updated = lax.dynamic_update_slice_in_dim(pooled_units, unit_rows, clipped * SENT_MB, 0)
        return jnp.where(active, updated, pooled_units)

    source = gathered_copies(hidden_in, "tensor", 1)

    def advance(step_index, loop_state):
        incoming, pooled_units = loop_state
        active, clipped = plan(step_index)
        entering = lax.dynamic_slice_in_dim(source, clipped * MB_TOK, MB_TOK, 0)
        current = jnp.where(section_index == 0, entering, incoming)
        wide_state = current.astype(jnp.float32)
        inv_rms = lax.rsqrt(jnp.mean(wide_state * wide_state, axis=1, keepdims=True) + RMS_EPS)
        normed = (wide_state * inv_rms * gain_full[None, :]).astype(jnp.bfloat16)
        gate_sum = jnp.dot(normed, gate_full, preferred_element_type=jnp.float32)
        up_sum = jnp.dot(normed, up_full, preferred_element_type=jnp.float32)
        hidden = (jax.nn.silu(gate_sum) * up_sum).astype(jnp.bfloat16)
        partial_value = lax.dot_general(
            hidden, down_full, CONTRACT_LAST, preferred_element_type=jnp.float32
        )
        reduced = sent_and_summed(partial_value.astype(jnp.bfloat16), "tensor", 1)
        residual_part = lax.dynamic_slice_in_dim(wide_state, tensor_index * columns, columns, 1)
        output_part = (residual_part + reduced).astype(jnp.bfloat16)
        output = gathered_copies(output_part, "tensor", 1)
        sentence_len = lax.dynamic_slice_in_dim(lengths, clipped * SENT_MB, SENT_MB, 0)
        pooled = pool_rows(output, sentence_len)
        centered = pooled - jnp.mean(pooled, axis=1, keepdims=True)
        unit_rows = (
            centered * lax.rsqrt(jnp.mean(centered * centered, axis=1, keepdims=True) + UNIT_FLOOR)
        ).astype(jnp.bfloat16)
        pooled_units = store_unit(pooled_units, unit_rows, active, clipped)
        incoming = passed_along(output, "section", 1)
        return (incoming, pooled_units)

    initial = (jnp.zeros((MB_TOK, D), jnp.bfloat16), jnp.zeros((SENT_DEV, D), jnp.bfloat16))
    leftover, pooled_units = lax.fori_loop(0, tick_count, advance, initial)
    everyone = gathered_copies(pooled_units, "dp", 0)
    products = lax.dot_general(
        pooled_units, everyone, CONTRACT_LAST, preferred_element_type=jnp.float32
    )
    return (1.0 - products / D)[None]


def solution(mesh):
    placed = (
        P("dp", "tensor"),
        P("section", None),
        P("section", "dp", "tensor"),
        P("section", "dp", "tensor"),
        P("section", "dp", "tensor"),
        P("dp"),
    )
    return jax.shard_map(
        per_device, mesh=mesh, in_specs=placed, out_specs=P("section", "dp", None), check_vma=False
    )
```

profile of v0, /device:TPU:7, one launch (start us, length us, event | category | flops | bytes accessed | tf_op | source)
XLA Modules:
  0.0 376.8 jit_solution(8650867605981222841)
XLA Ops:
  6.5 3.1 pad_maximum_fusion
  9.7 0.7 broadcast_in_dim.47
  10.4 9.2 %all-to-all-start.2 = ((bf16[16,32,256]{2,1,0:T(8,128)(2,1)}), bf16[16,32,256]{2,1,0:T(8,128)(2,1)S(1)}, u32[]{:S(2)}, u32[]{:S(2)}) async-start(bf16[16,32,256]{2,1,0:T(8,128)(2,1)} %broadcast_in_dim.47), calls=%async_computation.2 | async-start | bytes 524288 | tf_op jit(solution)/shard_map/all_to_all | solution.py:36
  19.6 11.6 %all-to-all-done.2 = bf16[16,32,256]{2,1,0:T(8,128)(2,1)S(1)} async-done(((bf16[16,32,256]{2,1,0:T(8,128)(2,1)}), bf16[16,32,256]{2,1,0:T(8,128)(2,1)S(1)}, u32[]{:S(2)}, u32[]{:S(2)}) %all-to-all-start.2) | async-done | bytes 262176 | tf_op jit(solution)/shard_map/all_to_all | solution.py:36
  31.2 102.5 %all-gather.2.cloned.1.call-done = bf16[4096,1536]{1,0:T(8,128)(2,1)} async-done(((bf16[1024,1536]{1,0:T(8,128)(2,1)}), bf16[4096,1536]{1,0:T(8,128)(2,1)}) %all-gather.2.cloned.1.call-update) | async-done | bytes 12582928 | tf_op jit(solution)/shard_map/all_gather | solution.py:25
  133.7 9.2 %fusion.15 = (bf16[4096,512]{1,0:T(8,128)(2,1)}, bf16[4096,512]{1,0:T(8,128)(2,1)}, bf16[4096,512]{1,0:T(8,128)(2,1)}) fusion(bf16[4096,1536]{1,0:T(8,128)(2,1)} %all-gather.2.cloned.1.call-done), kind=kLoop, calls=%fused_computation.35 | loop fusion | bytes 25165824 | tf_op jit(solution)/shard_map/split | solution.py:25
  143.0 217.9 %while.17 = (s32[]{:T(128)}, bf16[16,4096]{1,0:T(8,128)(2,1)S(1)}, bf16[4,4096]{1,0:T(4,128)(2,1)S(1)}, pred[]{:T(512)}, s32[]{:T(128)}, /*index=5*/bf16[32,4096...) while((s32[]{:T(128)}, bf16[16,4096]{1,0:T(8,128)(2,1)S(1)}, ...), condition=%wide.region_6.7_spmd, body=%wide.region_0.6_spmd.sunk | while | flops 202690624 | bytes 17926100 | solution.py:119
  143.2 2.9 fusion.33
  146.1 5.3 %convolution_convert_fusion.2 = bf16[16,4096]{1,0:T(8,128)(2,1)S(1)} fusion(bf16[4096,512]{1,0:T(8,128)(2,1)} %get-tuple-element.433, bf16[4096,512]{1,0:T(8,128)(2,1)} %get-tuple-element.432, f32[16,512]{1,0:T(8,128)S(1)} %fusion.33, f32[4096]{0:T(1024)S(1)} %bitcast.50, f32[16]{0:T(128)S(1)} %add_rsqrt_fusion.4, ...), kind=kOutput, calls=%fused_computation.clone.1 | convolution fusion | flops 134594560 | bytes 8699968 | tf_op jit(solution)/shard_map/while/body/eval_jaxpr/dot_general | solution.py:101
  151.4 0.7 copy.20
  152.0 7.9 %all-to-all-start = ((bf16[16,16,256]{2,1,0:T(8,128)(2,1)}), bf16[16,16,256]{2,1,0:T(8,128)(2,1)S(1)}, u32[]{:S(2)}, u32[]{:S(2)}) async-start(bf16[16,16,256]{2,1,0:T(8,128)(2,1)} %bitcast.42), calls=%async_computation | async-start | bytes 262144 | tf_op jit(solution)/shard_map/while/body/eval_jaxpr/all_to_all | solution.py:51
  159.9 8.9 %all-to-all-done = bf16[16,16,256]{2,1,0:T(8,128)(2,1)S(1)} async-done(((bf16[16,16,256]{2,1,0:T(8,128)(2,1)}), bf16[16,16,256]{2,1,0:T(8,128)(2,1)S(1)}, u32[]{:S(2)}, u32[]{:S(2)}) %all-to-all-start) | async-done | bytes 131104 | tf_op jit(solution)/shard_map/while/body/eval_jaxpr/all_to_all | solution.py:51
  168.8 0.7 broadcast_in_dim.51
  169.5 3.4 all-to-all-start.1
  173.1 8.8 %all-to-all-done.1 = bf16[16,16,256]{2,1,0:T(8,128)(2,1)S(1)} async-done(((bf16[16,16,256]{2,1,0:T(8,128)(2,1)}), bf16[16,16,256]{2,1,0:T(8,128)(2,1)S(1)}, u32[]{:S(2)}, u32[]{:S(2)}) %all-to-all-start.1) | async-done | bytes 131104 | tf_op jit(solution)/shard_map/while/body/eval_jaxpr/all_to_all | solution.py:36
  182.5 0.2 multiply_reduce_fusion.8
  182.7 1.3 collective-permute-start
  184.1 5.9 %collective-permute-done = bf16[16,4096]{1,0:T(8,128)(2,1)S(1)} collective-permute-done((bf16[16,4096]{1,0:T(8,128)(2,1)S(1)}, bf16[16,4096]{1,0:T(8,128)(2,1)S(1)}, u32[]{:S(2)}, u32[]{:S(2)}) %collective-permute-start) | collective-permute-done | bytes 131104 | tf_op jit(solution)/shard_map/while/body/eval_jaxpr/ppermute | solution.py:58
  190.2 2.9 fusion.33
  193.1 5.3 %convolution_convert_fusion.2 = bf16[16,4096]{1,0:T(8,128)(2,1)S(1)} fusion(bf16[4096,512]{1,0:T(8,128)(2,1)} %get-tuple-element.433, bf16[4096,512]{1,0:T(8,128)(2,1)} %get-tuple-element.432, f32[16,512]{1,0:T(8,128)S(1)} %fusion.33, f32[4096]{0:T(1024)S(1)} %bitcast.50, f32[16]{0:T(128)S(1)} %add_rsqrt_fusion.4, ...), kind=kOutput, calls=%fused_computation.clone.1 | convolution fusion | flops 134594560 | bytes 8699968 | tf_op jit(solution)/shard_map/while/body/eval_jaxpr/dot_general | solution.py:101
  198.4 0.7 copy.20
  199.0 3.8 %all-to-all-start = ((bf16[16,16,256]{2,1,0:T(8,128)(2,1)}), bf16[16,16,256]{2,1,0:T(8,128)(2,1)S(1)}, u32[]{:S(2)}, u32[]{:S(2)}) async-start(bf16[16,16,256]{2,1,0:T(8,128)(2,1)} %bitcast.42), calls=%async_computation | async-start | bytes 262144 | tf_op jit(solution)/shard_map/while/body/eval_jaxpr/all_to_all | solution.py:51
  202.9 9.2 %all-to-all-done = bf16[16,16,256]{2,1,0:T(8,128)(2,1)S(1)} async-done(((bf16[16,16,256]{2,1,0:T(8,128)(2,1)}), bf16[16,16,256]{2,1,0:T(8,128)(2,1)S(1)}, u32[]{:S(2)}, u32[]{:S(2)}) %all-to-all-start) | async-done | bytes 131104 | tf_op jit(solution)/shard_map/while/body/eval_jaxpr/all_to_all | solution.py:51
  212.1 0.7 broadcast_in_dim.51
  212.7 3.4 all-to-all-start.1
  216.3 8.3 %all-to-all-done.1 = bf16[16,16,256]{2,1,0:T(8,128)(2,1)S(1)} async-done(((bf16[16,16,256]{2,1,0:T(8,128)(2,1)}), bf16[16,16,256]{2,1,0:T(8,128)(2,1)S(1)}, u32[]{:S(2)}, u32[]{:S(2)}) %all-to-all-start.1) | async-done | bytes 131104 | tf_op jit(solution)/shard_map/while/body/eval_jaxpr/all_to_all | solution.py:36
  225.2 0.2 multiply_reduce_fusion.8
  225.5 1.3 collective-permute-start
  226.9 5.6 %collective-permute-done = bf16[16,4096]{1,0:T(8,128)(2,1)S(1)} collective-permute-done((bf16[16,4096]{1,0:T(8,128)(2,1)S(1)}, bf16[16,4096]{1,0:T(8,128)(2,1)S(1)}, u32[]{:S(2)}, u32[]{:S(2)}) %collective-permute-start) | collective-permute-done | bytes 131104 | tf_op jit(solution)/shard_map/while/body/eval_jaxpr/ppermute | solution.py:58
  232.7 2.9 fusion.33
  235.6 5.3 %convolution_convert_fusion.2 = bf16[16,4096]{1,0:T(8,128)(2,1)S(1)} fusion(bf16[4096,512]{1,0:T(8,128)(2,1)} %get-tuple-element.433, bf16[4096,512]{1,0:T(8,128)(2,1)} %get-tuple-element.432, f32[16,512]{1,0:T(8,128)S(1)} %fusion.33, f32[4096]{0:T(1024)S(1)} %bitcast.50, f32[16]{0:T(128)S(1)} %add_rsqrt_fusion.4, ...), kind=kOutput, calls=%fused_computation.clone.1 | convolution fusion | flops 134594560 | bytes 8699968 | tf_op jit(solution)/shard_map/while/body/eval_jaxpr/dot_general | solution.py:101
  240.9 0.7 copy.20
  241.5 4.1 %all-to-all-start = ((bf16[16,16,256]{2,1,0:T(8,128)(2,1)}), bf16[16,16,256]{2,1,0:T(8,128)(2,1)S(1)}, u32[]{:S(2)}, u32[]{:S(2)}) async-start(bf16[16,16,256]{2,1,0:T(8,128)(2,1)} %bitcast.42), calls=%async_computation | async-start | bytes 262144 | tf_op jit(solution)/shard_map/while/body/eval_jaxpr/all_to_all | solution.py:51
  245.6 9.2 %all-to-all-done = bf16[16,16,256]{2,1,0:T(8,128)(2,1)S(1)} async-done(((bf16[16,16,256]{2,1,0:T(8,128)(2,1)}), bf16[16,16,256]{2,1,0:T(8,128)(2,1)S(1)}, u32[]{:S(2)}, u32[]{:S(2)}) %all-to-all-start) | async-done | bytes 131104 | tf_op jit(solution)/shard_map/while/body/eval_jaxpr/all_to_all | solution.py:51
  254.9 0.7 broadcast_in_dim.51
  255.5 3.4 all-to-all-start.1
  259.1 8.3 %all-to-all-done.1 = bf16[16,16,256]{2,1,0:T(8,128)(2,1)S(1)} async-done(((bf16[16,16,256]{2,1,0:T(8,128)(2,1)}), bf16[16,16,256]{2,1,0:T(8,128)(2,1)S(1)}, u32[]{:S(2)}, u32[]{:S(2)}) %all-to-all-start.1) | async-done | bytes 131104 | tf_op jit(solution)/shard_map/while/body/eval_jaxpr/all_to_all | solution.py:36
  268.0 0.2 multiply_reduce_fusion.8
  268.3 1.3 collective-permute-start
  269.7 5.6 %collective-permute-done = bf16[16,4096]{1,0:T(8,128)(2,1)S(1)} collective-permute-done((bf16[16,4096]{1,0:T(8,128)(2,1)S(1)}, bf16[16,4096]{1,0:T(8,128)(2,1)S(1)}, u32[]{:S(2)}, u32[]{:S(2)}) %collective-permute-start) | collective-permute-done | bytes 131104 | tf_op jit(solution)/shard_map/while/body/eval_jaxpr/ppermute | solution.py:58
  275.5 2.9 fusion.33
  278.4 5.3 %convolution_convert_fusion.2 = bf16[16,4096]{1,0:T(8,128)(2,1)S(1)} fusion(bf16[4096,512]{1,0:T(8,128)(2,1)} %get-tuple-element.433, bf16[4096,512]{1,0:T(8,128)(2,1)} %get-tuple-element.432, f32[16,512]{1,0:T(8,128)S(1)} %fusion.33, f32[4096]{0:T(1024)S(1)} %bitcast.50, f32[16]{0:T(128)S(1)} %add_rsqrt_fusion.4, ...), kind=kOutput, calls=%fused_computation.clone.1 | convolution fusion | flops 134594560 | bytes 8699968 | tf_op jit(solution)/shard_map/while/body/eval_jaxpr/dot_general | solution.py:101
  283.7 0.7 copy.20
  284.3 4.1 %all-to-all-start = ((bf16[16,16,256]{2,1,0:T(8,128)(2,1)}), bf16[16,16,256]{2,1,0:T(8,128)(2,1)S(1)}, u32[]{:S(2)}, u32[]{:S(2)}) async-start(bf16[16,16,256]{2,1,0:T(8,128)(2,1)} %bitcast.42), calls=%async_computation | async-start | bytes 262144 | tf_op jit(solution)/shard_map/while/body/eval_jaxpr/all_to_all | solution.py:51
  288.4 9.2 %all-to-all-done = bf16[16,16,256]{2,1,0:T(8,128)(2,1)S(1)} async-done(((bf16[16,16,256]{2,1,0:T(8,128)(2,1)}), bf16[16,16,256]{2,1,0:T(8,128)(2,1)S(1)}, u32[]{:S(2)}, u32[]{:S(2)}) %all-to-all-start) | async-done | bytes 131104 | tf_op jit(solution)/shard_map/while/body/eval_jaxpr/all_to_all | solution.py:51
  297.6 0.7 broadcast_in_dim.51
  298.3 3.4 all-to-all-start.1
  301.9 8.3 %all-to-all-done.1 = bf16[16,16,256]{2,1,0:T(8,128)(2,1)S(1)} async-done(((bf16[16,16,256]{2,1,0:T(8,128)(2,1)}), bf16[16,16,256]{2,1,0:T(8,128)(2,1)S(1)}, u32[]{:S(2)}, u32[]{:S(2)}) %all-to-all-start.1) | async-done | bytes 131104 | tf_op jit(solution)/shard_map/while/body/eval_jaxpr/all_to_all | solution.py:36
  310.8 0.2 multiply_reduce_fusion.8
  311.0 1.3 collective-permute-start
  312.4 5.6 %collective-permute-done = bf16[16,4096]{1,0:T(8,128)(2,1)S(1)} collective-permute-done((bf16[16,4096]{1,0:T(8,128)(2,1)S(1)}, bf16[16,4096]{1,0:T(8,128)(2,1)S(1)}, u32[]{:S(2)}, u32[]{:S(2)}) %collective-permute-start) | collective-permute-done | bytes 131104 | tf_op jit(solution)/shard_map/while/body/eval_jaxpr/ppermute | solution.py:58
  318.3 2.9 fusion.33
  321.1 5.3 %convolution_convert_fusion.2 = bf16[16,4096]{1,0:T(8,128)(2,1)S(1)} fusion(bf16[4096,512]{1,0:T(8,128)(2,1)} %get-tuple-element.433, bf16[4096,512]{1,0:T(8,128)(2,1)} %get-tuple-element.432, f32[16,512]{1,0:T(8,128)S(1)} %fusion.33, f32[4096]{0:T(1024)S(1)} %bitcast.50, f32[16]{0:T(128)S(1)} %add_rsqrt_fusion.4, ...), kind=kOutput, calls=%fused_computation.clone.1 | convolution fusion | flops 134594560 | bytes 8699968 | tf_op jit(solution)/shard_map/while/body/eval_jaxpr/dot_general | solution.py:101
  326.4 0.7 copy.20
  327.1 4.1 %all-to-all-start = ((bf16[16,16,256]{2,1,0:T(8,128)(2,1)}), bf16[16,16,256]{2,1,0:T(8,128)(2,1)S(1)}, u32[]{:S(2)}, u32[]{:S(2)}) async-start(bf16[16,16,256]{2,1,0:T(8,128)(2,1)} %bitcast.42), calls=%async_computation | async-start | bytes 262144 | tf_op jit(solution)/shard_map/while/body/eval_jaxpr/all_to_all | solution.py:51
  331.2 9.2 %all-to-all-done = bf16[16,16,256]{2,1,0:T(8,128)(2,1)S(1)} async-done(((bf16[16,16,256]{2,1,0:T(8,128)(2,1)}), bf16[16,16,256]{2,1,0:T(8,128)(2,1)S(1)}, u32[]{:S(2)}, u32[]{:S(2)}) %all-to-all-start) | async-done | bytes 131104 | tf_op jit(solution)/shard_map/while/body/eval_jaxpr/all_to_all | solution.py:51
  340.4 0.7 broadcast_in_dim.51
  341.1 3.4 all-to-all-start.1
  344.6 8.3 %all-to-all-done.1 = bf16[16,16,256]{2,1,0:T(8,128)(2,1)S(1)} async-done(((bf16[16,16,256]{2,1,0:T(8,128)(2,1)}), bf16[16,16,256]{2,1,0:T(8,128)(2,1)S(1)}, u32[]{:S(2)}, u32[]{:S(2)}) %all-to-all-start.1) | async-done | bytes 131104 | tf_op jit(solution)/shard_map/while/body/eval_jaxpr/all_to_all | solution.py:36
  353.6 0.2 multiply_reduce_fusion.8
  353.8 1.3 collective-permute-start
  355.2 5.6 %collective-permute-done = bf16[16,4096]{1,0:T(8,128)(2,1)S(1)} collective-permute-done((bf16[16,4096]{1,0:T(8,128)(2,1)S(1)}, bf16[16,4096]{1,0:T(8,128)(2,1)S(1)}, u32[]{:S(2)}, u32[]{:S(2)}) %collective-permute-start) | collective-permute-done | bytes 131104 | tf_op jit(solution)/shard_map/while/body/eval_jaxpr/ppermute | solution.py:58
  360.9 8.3 %all_to_all.34 = bf16[4,4,4096]{2,1,0:T(4,128)(2,1)S(1)} all-to-all(bf16[4,4,4096]{2,1,0:T(4,128)(2,1)S(1)} %broadcast_in_dim.48), channel_id=1, replica_groups=mesh['section'=4,'tensor'=16,'dp'=4] {'dp'}, dimensions={0} | all-to-all | bytes 262144 | tf_op jit(solution)/shard_map/all_to_all | solution.py:36
  369.2 0.7 fusion.11
  (93 shorter events, 5.7 us)
Async XLA Ops:
  6.5 127.1 %all-gather.2.cloned.1.call-start = ((), (), s32[]{:S(2)}) async-start(), calls=%async_computation.4 | async-start | bytes 15728640 | tf_op jit(solution)/shard_map/all_gather | solution.py:25
  6.5 3.1 copy-start.1
  10.4 20.7 %all-to-all-start.2 = ((bf16[16,32,256]{2,1,0:T(8,128)(2,1)}), bf16[16,32,256]{2,1,0:T(8,128)(2,1)S(1)}, u32[]{:S(2)}, u32[]{:S(2)}) async-start(bf16[16,32,256]{2,1,0:T(8,128)(2,1)} %broadcast_in_dim.47), calls=%async_computation.2 | async-start | bytes 524288 | tf_op jit(solution)/shard_map/all_to_all | solution.py:36
  31.2 111.8 %copy-start = (f32[1,4096]{1,0:T(1,128)S(1)}, f32[1,4096]{1,0:T(1,128)}, u32[]{:S(2)}) copy-start(f32[1,4096]{1,0:T(1,128)} %param.9) | copy-start | bytes 49156
  31.2 111.8 %copy-start.2 = (s32[4]{0:T(128)S(1)}, s32[4]{0:T(128)}, u32[]{:S(2)}) copy-start(s32[4]{0:T(128)} %param.13) | copy-start | bytes 52
  152.0 16.8 %all-to-all-start = ((bf16[16,16,256]{2,1,0:T(8,128)(2,1)}), bf16[16,16,256]{2,1,0:T(8,128)(2,1)S(1)}, u32[]{:S(2)}, u32[]{:S(2)}) async-start(bf16[16,16,256]{2,1,0:T(8,128)(2,1)} %bitcast.42), calls=%async_computation | async-start | bytes 262144 | tf_op jit(solution)/shard_map/while/body/eval_jaxpr/all_to_all | solution.py:51
  169.5 12.3 %all-to-all-start.1 = ((bf16[16,16,256]{2,1,0:T(8,128)(2,1)}), bf16[16,16,256]{2,1,0:T(8,128)(2,1)S(1)}, u32[]{:S(2)}, u32[]{:S(2)}) async-start(bf16[16,16,256]{2,1,0:T(8,128)(2,1)} %broadcast_in_dim.51), calls=%async_computation.1 | async-start | bytes 262144 | tf_op jit(solution)/shard_map/while/body/eval_jaxpr/all_to_all | solution.py:36
  182.7 7.3 %collective-permute-start = (bf16[16,4096]{1,0:T(8,128)(2,1)S(1)}, bf16[16,4096]{1,0:T(8,128)(2,1)S(1)}, u32[]{:S(2)}, u32[]{:S(2)}) collective-permute-start(bf16[16,4096]{1,0:T(8,128)(2,1)S(1)} %bitcast.47), channel_id=1, source_target_pairs={{0,64},{64,128},{128,192},{1,65},{65,129},{129,193},{2,66},{66,130... | collective-permute-start | bytes 393224 | tf_op jit(solution)/shard_map/while/body/eval_jaxpr/ppermute | solution.py:58
  199.0 13.0 %all-to-all-start = ((bf16[16,16,256]{2,1,0:T(8,128)(2,1)}), bf16[16,16,256]{2,1,0:T(8,128)(2,1)S(1)}, u32[]{:S(2)}, u32[]{:S(2)}) async-start(bf16[16,16,256]{2,1,0:T(8,128)(2,1)} %bitcast.42), calls=%async_computation | async-start | bytes 262144 | tf_op jit(solution)/shard_map/while/body/eval_jaxpr/all_to_all | solution.py:51
  212.7 11.9 %all-to-all-start.1 = ((bf16[16,16,256]{2,1,0:T(8,128)(2,1)}), bf16[16,16,256]{2,1,0:T(8,128)(2,1)S(1)}, u32[]{:S(2)}, u32[]{:S(2)}) async-start(bf16[16,16,256]{2,1,0:T(8,128)(2,1)} %broadcast_in_dim.51), calls=%async_computation.1 | async-start | bytes 262144 | tf_op jit(solution)/shard_map/while/body/eval_jaxpr/all_to_all | solution.py:36
  225.5 7.0 %collective-permute-start = (bf16[16,4096]{1,0:T(8,128)(2,1)S(1)}, bf16[16,4096]{1,0:T(8,128)(2,1)S(1)}, u32[]{:S(2)}, u32[]{:S(2)}) collective-permute-start(bf16[16,4096]{1,0:T(8,128)(2,1)S(1)} %bitcast.47), channel_id=1, source_target_pairs={{0,64},{64,128},{128,192},{1,65},{65,129},{129,193},{2,66},{66,130... | collective-permute-start | bytes 393224 | tf_op jit(solution)/shard_map/while/body/eval_jaxpr/ppermute | solution.py:58
  241.5 13.3 %all-to-all-start = ((bf16[16,16,256]{2,1,0:T(8,128)(2,1)}), bf16[16,16,256]{2,1,0:T(8,128)(2,1)S(1)}, u32[]{:S(2)}, u32[]{:S(2)}) async-start(bf16[16,16,256]{2,1,0:T(8,128)(2,1)} %bitcast.42), calls=%async_computation | async-start | bytes 262144 | tf_op jit(solution)/shard_map/while/body/eval_jaxpr/all_to_all | solution.py:51
  255.5 11.9 %all-to-all-start.1 = ((bf16[16,16,256]{2,1,0:T(8,128)(2,1)}), bf16[16,16,256]{2,1,0:T(8,128)(2,1)S(1)}, u32[]{:S(2)}, u32[]{:S(2)}) async-start(bf16[16,16,256]{2,1,0:T(8,128)(2,1)} %broadcast_in_dim.51), calls=%async_computation.1 | async-start | bytes 262144 | tf_op jit(solution)/shard_map/while/body/eval_jaxpr/all_to_all | solution.py:36
  268.3 7.0 %collective-permute-start = (bf16[16,4096]{1,0:T(8,128)(2,1)S(1)}, bf16[16,4096]{1,0:T(8,128)(2,1)S(1)}, u32[]{:S(2)}, u32[]{:S(2)}) collective-permute-start(bf16[16,4096]{1,0:T(8,128)(2,1)S(1)} %bitcast.47), channel_id=1, source_target_pairs={{0,64},{64,128},{128,192},{1,65},{65,129},{129,193},{2,66},{66,130... | collective-permute-start | bytes 393224 | tf_op jit(solution)/shard_map/while/body/eval_jaxpr/ppermute | solution.py:58
  284.3 13.3 %all-to-all-start = ((bf16[16,16,256]{2,1,0:T(8,128)(2,1)}), bf16[16,16,256]{2,1,0:T(8,128)(2,1)S(1)}, u32[]{:S(2)}, u32[]{:S(2)}) async-start(bf16[16,16,256]{2,1,0:T(8,128)(2,1)} %bitcast.42), calls=%async_computation | async-start | bytes 262144 | tf_op jit(solution)/shard_map/while/body/eval_jaxpr/all_to_all | solution.py:51
  298.3 11.9 %all-to-all-start.1 = ((bf16[16,16,256]{2,1,0:T(8,128)(2,1)}), bf16[16,16,256]{2,1,0:T(8,128)(2,1)S(1)}, u32[]{:S(2)}, u32[]{:S(2)}) async-start(bf16[16,16,256]{2,1,0:T(8,128)(2,1)} %broadcast_in_dim.51), calls=%async_computation.1 | async-start | bytes 262144 | tf_op jit(solution)/shard_map/while/body/eval_jaxpr/all_to_all | solution.py:36
  311.0 7.0 %collective-permute-start = (bf16[16,4096]{1,0:T(8,128)(2,1)S(1)}, bf16[16,4096]{1,0:T(8,128)(2,1)S(1)}, u32[]{:S(2)}, u32[]{:S(2)}) collective-permute-start(bf16[16,4096]{1,0:T(8,128)(2,1)S(1)} %bitcast.47), channel_id=1, source_target_pairs={{0,64},{64,128},{128,192},{1,65},{65,129},{129,193},{2,66},{66,130... | collective-permute-start | bytes 393224 | tf_op jit(solution)/shard_map/while/body/eval_jaxpr/ppermute | solution.py:58
  327.1 13.3 %all-to-all-start = ((bf16[16,16,256]{2,1,0:T(8,128)(2,1)}), bf16[16,16,256]{2,1,0:T(8,128)(2,1)S(1)}, u32[]{:S(2)}, u32[]{:S(2)}) async-start(bf16[16,16,256]{2,1,0:T(8,128)(2,1)} %bitcast.42), calls=%async_computation | async-start | bytes 262144 | tf_op jit(solution)/shard_map/while/body/eval_jaxpr/all_to_all | solution.py:51
  341.1 11.9 %all-to-all-start.1 = ((bf16[16,16,256]{2,1,0:T(8,128)(2,1)}), bf16[16,16,256]{2,1,0:T(8,128)(2,1)S(1)}, u32[]{:S(2)}, u32[]{:S(2)}) async-start(bf16[16,16,256]{2,1,0:T(8,128)(2,1)} %broadcast_in_dim.51), calls=%async_computation.1 | async-start | bytes 262144 | tf_op jit(solution)/shard_map/while/body/eval_jaxpr/all_to_all | solution.py:36
  353.8 7.0 %collective-permute-start = (bf16[16,4096]{1,0:T(8,128)(2,1)S(1)}, bf16[16,4096]{1,0:T(8,128)(2,1)S(1)}, u32[]{:S(2)}, u32[]{:S(2)}) collective-permute-start(bf16[16,4096]{1,0:T(8,128)(2,1)S(1)} %bitcast.47), channel_id=1, source_target_pairs={{0,64},{64,128},{128,192},{1,65},{65,129},{129,193},{2,66},{66,130... | collective-permute-start | bytes 393224 | tf_op jit(solution)/shard_map/while/body/eval_jaxpr/ppermute | solution.py:58
Sparse Core Ops, SparseCore 0:
  9.8 123.8 all-gather.1
where the time goes:
time: 380 us; the launch traced here: 377 us
  waiting for transfers between devices  230 us (61%)
  starting transfers between devices  56.6 us (15%)
  matrix products  41.6 us (11%)
  local copies, waits for them, and re-layouts  17.8 us (5%)
  between operations  13.5 us (4%)
  other arithmetic  8.68 us (2%)
  blocking collectives  8.34 us (2%)
    all_gather x1, waiting for transfers between devices, side_by_side(): lax.all_gather(both, axis, axis=dim, tiled=True)  102 us
    all_to_all x6, waiting for transfers between devices, sent_to_all(): return lax.all_to_all(copies, axis, split_axis=0, concat_axis=0, tiled=True)  53.5 us
    all_to_all x5, waiting for transfers between devices, sent_and_summed(): lax.all_to_all(in_blocks(array, dim, peers), axis, 0, 0, tiled=True)  45.6 us
    ppermute x5, waiting for transfers between devices, passed_along(): return lax.ppermute(array, axis, pairs)  28.3 us
    dot_general x5, matrix products, advance(): lax.dot_general(hidden, down_full, CONTRACT_LAST, preferred_element_type=...  26.4 us
    all_to_all x6, starting transfers between devices, sent_to_all(): return lax.all_to_all(copies, axis, split_axis=0, concat_axis=0, tiled=True)  26.2 us
    all_to_all x5, starting transfers between devices, sent_and_summed(): lax.all_to_all(in_blocks(array, dim, peers), axis, 0, 0, tiled=True)  23.9 us
    dot_general x5, matrix products, advance(): gate_sum = jnp.dot(normed, gate_full, preferred_element_type=jnp.float32)  14.4 us
  transfers between devices with their start and end apart: 17, of which 17 were waited for; matrix products, arithmetic and copies ran while one was open for 1% of the time, Pallas kernels for 0%

commit v1 on v0

v1 whole, which is shorter than its diff:
```python
import jax
import jax.numpy as jnp
from jax import lax
from jax.experimental import pallas as pl
from jax.experimental.pallas import tpu as pltpu
from jax.sharding import PartitionSpec as P

D = 4096
LEN = 8
SENT = 16
NY = 4
NZ = 8
NS = 4
ROWS = D // NY
FFC = 1024
SUB = FFC // NY
COL = ROWS // NZ
GROUP = 64
K = 2
T = GROUP // K
SPC = T // LEN
PARTS = 32 // T
RMS_EPS = 1e-05
UNIT_FLOOR = 0.1
NT = (((1,), (1,)), ((), ()))
MESH = pl.DeviceIdType.MESH
F32 = jnp.float32
BF16 = jnp.bfloat16


def kernel(
    hid_in, gain_in, gate_in, up_in, down_in, len_in, out_ref,
    hv, gv, wg, wu, wd, xb, ps, pr, sr, hr, zs, zr, yo, wl, pv, gz, gy, fs,
    in_sem, w_sem, wsend, wrecv, dsend, xsem, psend, prsem, ssend, srsem,
    hsend, hrsem, zsend, zrsem, ysend, lsend, lrsem, csend, crsem, gzsend, gzsem, gysend, gysem,
):
    s = lax.axis_index("section")
    t = lax.axis_index("tensor")
    y = lax.axis_index("dp")
    z = t // 2
    c = t % 2

    def at(sec, zz, cc, yy):
        return {"section": sec, "tensor": zz * 2 + cc, "dp": yy}

    def remote(src, dst, ssem, rsem, dev):
        return pltpu.make_async_remote_copy(
            src_ref=src, dst_ref=dst, send_sem=ssem, recv_sem=rsem, device_id=dev, device_id_type=MESH
        )

    me = at(s, z, c, y)

    hid_cp = pltpu.make_async_copy(hid_in, hv, in_sem.at[0])
    hid_cp.start()
    gain_cp = pltpu.make_async_copy(
        gain_in.at[:, pl.ds(pl.multiple_of(y * ROWS, ROWS), ROWS)], gv, in_sem.at[1]
    )
    loads = []
    for i in range(2):
        loads.append(pltpu.make_async_copy(gate_in.at[0, :, pl.ds(SUB * i, SUB)], wg.at[2 * c + i], w_sem.at[i]))
        loads.append(pltpu.make_async_copy(up_in.at[0, :, pl.ds(SUB * i, SUB)], wu.at[2 * c + i], w_sem.at[2 + i]))
    loads.append(pltpu.make_async_copy(down_in, wd.at[c], w_sem.at[4]))
    for cp in loads:
        cp.start()
    gain_cp.start()

    barrier = pltpu.get_barrier_semaphore()

    def greet(dev):
        pl.semaphore_signal(barrier, inc=1, device_id=dev, device_id_type=MESH)

    first = s == 0
    last = s == NS - 1
    src_y = 2 * c
    self_feed = jnp.logical_and(y == z // 2, c == y // 2)

    @pl.when(first)
    def _():
        def feed_greet(i, carry):
            @pl.when(jnp.logical_not(jnp.logical_and(self_feed, i == z)))
            def _():
                greet(at(s, i, y // 2, z // 2))

            sy = src_y + i // 4
            sz = 2 * y + (i // 2) % 2
            sc = i % 2

            @pl.when(jnp.logical_not(jnp.logical_and(sy == y, jnp.logical_and(sz == z, sc == c))))
            def _():
                greet(at(s, sz, sc, sy))

            return carry

        lax.fori_loop(0, NZ, feed_greet, 0)

    def z_greet(i, carry):
        @pl.when(i > 0)
        def _():
            greet(at(s, (z + i) % NZ, c, y))

        @pl.when(s > 0)
        def _():
            greet(at(s - 1, (z + i) % NZ, c, y))

        @pl.when(s < NS - 1)
        def _():
            greet(at(s + 1, (z + i) % NZ, c, y))

        return carry

    lax.fori_loop(0, NZ, z_greet, 0)
    for d in range(1, NY):
        greet(at(s, z, c, (y + d) % NY))
    greet(at(s, z, 1 - c, y))
    own_feed = jnp.where(self_feed, 1, 0)
    peers = 1 + (NY - 1) + (NZ - 1)
    peers = peers + jnp.where(s > 0, NZ, 0) + jnp.where(s < NS - 1, NZ, 0)
    peers = peers + jnp.where(first, 2 * NZ - 2 * own_feed, 0)

    pos = lax.broadcasted_iota(jnp.int32, (LEN, 128), 0)
    for i in range(SENT // NY):
        n = len_in[i]
        wl[y * (SENT // NY) + i] = jnp.where(pos < n, 1.0 / jnp.full((LEN, 128), n, jnp.int32).astype(F32), 0.0)

    hid_cp.wait()
    pl.semaphore_wait(barrier, peers)

    @pl.when(first)
    def _():
        def feed(i, carry):
            zz = (z + NZ // 2 + i) % NZ
            for q in range(PARTS):
                for h in range(2):
                    src = hv.at[pl.ds(q * T, T), pl.ds(COL * h, COL)]
                    k = (y % 2) * PARTS + q
                    j = (z % 2) * 4 + c * 2 + h
                    dst = xb.at[k, j]
                    n = q * 2 + h

                    @pl.when(jnp.logical_and(self_feed, zz == z))
                    def _():
                        pltpu.make_async_copy(src, dst, xsem.at[k, j]).start()

                    @pl.when(jnp.logical_not(jnp.logical_and(self_feed, zz == z)))
                    def _():
                        remote(src, dst, dsend.at[i, n], xsem.at[k, j], at(s, zz, y // 2, z // 2)).start()

            return carry

        lax.fori_loop(0, NZ, feed, 0)

    for cp in loads:
        cp.wait()
    partner = at(s, z, 1 - c, y)
    swaps = [
        remote(wg.at[pl.ds(2 * c, 2)], wg.at[pl.ds(2 * c, 2)], wsend.at[0], wrecv.at[0], partner),
        remote(wu.at[pl.ds(2 * c, 2)], wu.at[pl.ds(2 * c, 2)], wsend.at[1], wrecv.at[1], partner),
        remote(wd.at[c], wd.at[c], wsend.at[2], wrecv.at[2], partner),
    ]
    for cp in swaps:
        cp.start()

    mine = wl.at[pl.ds(y * (SENT // NY), SENT // NY)]
    for d in range(1, NY):
        remote(mine, mine, lsend.at[d], lrsem.at[y], at(s, z, c, (y + d) % NY)).start()

    gain_cp.wait()
    swaps[0].wait_recv()
    swaps[1].wait_recv()

    lane_t = lax.broadcasted_iota(jnp.int32, (T, 128), 1)
    row_t = lax.broadcasted_iota(jnp.int32, (T, 128), 0)
    eye_t = lane_t == row_t

    def stage1(k):
        for j in range(NZ):
            remote(xb.at[k, j], xb.at[k, j], dsend.at[0, 0], xsem.at[k, j], me).wait_recv()
        x = jnp.concatenate([xb[k, j] for j in range(NZ)], axis=1).astype(F32)
        square = jnp.sum(x * x, axis=1, keepdims=True)
        sr[k, y] = jnp.sum(jnp.where(eye_t, square, 0.0), axis=0, keepdims=True)
        xg = (x * gv[...]).astype(BF16)
        for n, d in enumerate((2, 1, 3, 0)):
            yb = (y + d) % NY
            gate = jnp.dot(xg, wg[yb], preferred_element_type=F32)
            up = jnp.dot(xg, wu[yb], preferred_element_type=F32)
            both = jnp.concatenate([gate, up], axis=1).astype(BF16)
            if d == 0:
                pr[k, y] = both
            else:
                ps[k, d - 1] = both
                dev = at(s, z, c, yb)
                remote(sr.at[k, y], sr.at[k, y], ssend.at[k, d], srsem.at[k, y], dev).start()
                remote(ps.at[k, d - 1], pr.at[k, y], psend.at[k, d], prsem.at[k, y], dev).start()

    def stage2(k):
        for d in range(1, NY):
            src = (y + d) % NY
            remote(sr.at[k, src], sr.at[k, src], ssend.at[k, d], srsem.at[k, src], me).wait_recv()
            remote(pr.at[k, src], pr.at[k, src], psend.at[k, d], prsem.at[k, src], me).wait_recv()
        row = sr[k, 0] + sr[k, 1] + sr[k, 2] + sr[k, 3]
        square = jnp.sum(jnp.where(eye_t, row, 0.0), axis=1, keepdims=True)
        inv = lax.rsqrt(square * (1.0 / D) + RMS_EPS)
        total = pr[k, 0].astype(F32) + pr[k, 1].astype(F32) + pr[k, 2].astype(F32) + pr[k, 3].astype(F32)
        total = total * inv
        gate = total[:, :SUB]
        up = total[:, SUB:]
        hr[k, y] = (gate / (1.0 + jnp.exp(-gate)) * up).astype(BF16)
        for d in (2, 1, 3):
            remote(hr.at[k, y], hr.at[k, y], hsend.at[k, d], hrsem.at[k, y], at(s, z, c, (y + d) % NY)).start()

    def stage3(k):
        for d in range(1, NY):
            src = (y + d) % NY
            remote(hr.at[k, src], hr.at[k, src], hsend.at[k, d], hrsem.at[k, src], me).wait_recv()
        left = jnp.concatenate([hr[k, 0], hr[k, 1]], axis=1)
        right = jnp.concatenate([hr[k, 2], hr[k, 3]], axis=1)
        for d in (2, 1, 3, 0):
            p = (z // 2 + d) % 4
            part = lax.dot_general(left, wd[0, p], NT, preferred_element_type=F32)
            part += lax.dot_general(right, wd[1, p], NT, preferred_element_type=F32)
            part = part.astype(BF16)
            for i in range(2):
                j = 2 * p + i
                piece = part[:, COL * i : COL * (i + 1)]

                def send():
                    zs[k, j] = piece
                    remote(zs.at[k, j], zr.at[k, z], zsend.at[k, j], zrsem.at[k, z], at(s, j, c, y)).start()

                if d != 0:
                    send()
                else:

                    @pl.when(j == z)
                    def _():
                        zr[k, z] = piece

                    pl.when(j != z)(send)

    def stage4(k):
        for d in range(1, NZ):
            src = (z + d) % NZ
            remote(zr.at[k, src], zr.at[k, src], zsend.at[k, 0], zrsem.at[k, src], me).wait_recv()
        total = xb[k, z].astype(F32)
        for j in range(NZ):
            total += zr[k, j].astype(F32)
        state = total.astype(BF16)
        yo[k] = state

        @pl.when(s < NS - 1)
        def _():
            for d in (4, 3, 5, 2, 6, 1, 7, 0):
                zz = (z + d) % NZ
                remote(yo.at[k], xb.at[k, z], ysend.at[k, d], xsem.at[k, z], at(s + 1, zz, c, y)).start()

        weights = wl[pl.ds(c * (SENT // 2) + k * SPC, SPC)]
        pooled = jnp.sum(state.astype(F32).reshape(SPC, LEN, COL) * weights, axis=1)
        pv[c, pl.ds(k * SPC, SPC), :] = pooled

    for k in range(K):
        stage1(k)
    for k in range(K):
        stage2(k)
    swaps[2].wait_recv()
    for k in range(K):
        stage3(k)
    for d in range(1, NY):
        src = (y + d) % NY
        theirs = wl.at[pl.ds(src * (SENT // NY), SENT // NY)]
        remote(theirs, theirs, lsend.at[d], lrsem.at[src], me).wait_recv()
    for k in range(K):
        stage4(k)

    remote(pv.at[c], pv.at[c], csend, crsem, partner).start()
    remote(pv.at[1 - c], pv.at[1 - c], csend, crsem, partner).wait_recv()
    points = jnp.concatenate([pv[0], pv[1]], axis=0)
    mean = jnp.mean(points, axis=1, keepdims=True)
    points = points - mean
    padded = jnp.concatenate([points, jnp.zeros((128 - SENT, COL), F32)], axis=0)
    gram = lax.dot_general(points, padded, NT, precision=lax.Precision.HIGHEST, preferred_element_type=F32)
    lane = lax.broadcasted_iota(jnp.int32, (SENT, 128), 1)
    rowi = lax.broadcasted_iota(jnp.int32, (SENT, 128), 0)
    gz[z] = gram + jnp.where(lane == 32 + y * NZ + z, mean, 0.0)
    for d in (4, 3, 5, 2, 6, 1, 7):
        remote(gz.at[z], gz.at[z], gzsend.at[d], gzsem.at[z], at(s, (z + d) % NZ, c, y)).start()
    for d in range(1, NZ):
        src = (z + d) % NZ
        remote(gz.at[src], gz.at[src], gzsend.at[d], gzsem.at[src], me).wait_recv()
    sums = gz[0]
    for j in range(1, NZ):
        sums += gz[j]
    gy[y] = sums
    for d in (2, 1, 3):
        remote(gy.at[y], gy.at[y], gysend.at[d], gysem.at[y], at(s, z, c, (y + d) % NY)).start()
    for d in range(1, NY):
        src = (y + d) % NY
        remote(gy.at[src], gy.at[src], gysend.at[d], gysem.at[src], me).wait_recv()
    sums = gy[0] + gy[1] + gy[2] + gy[3]
    blocks = NY * NZ
    held = jnp.logical_and(lane >= 32, lane < 32 + blocks)
    means = jnp.where(held, sums, 0.0)
    means = jnp.where(held, means - jnp.sum(means, axis=1, keepdims=True) * (1.0 / blocks), 0.0)
    means_padded = jnp.concatenate([means, jnp.zeros((128 - SENT, 128), F32)], axis=0)
    cross = lax.dot_general(means, means_padded, NT, precision=lax.Precision.HIGHEST, preferred_element_type=F32)
    cov = (sums + COL * cross) * (1.0 / D)
    eye = lane == rowi
    scale = lax.rsqrt(jnp.sum(jnp.where(eye, cov, 0.0), axis=1, keepdims=True) + UNIT_FLOOR)
    scale_row = jnp.sum(jnp.where(eye, scale, 0.0), axis=0, keepdims=True)
    rdm = 1.0 - cov * scale * scale_row
    for i in range(NY):
        fs[i] = rdm[4 * i : 4 * i + 4]
    out_ref[0] = fs[y][:, :SENT]

    def sent(ref, sem):
        remote(ref, ref, sem, sem, partner).wait_send()

    @pl.when(first)
    def _():
        def drain(i, carry):
            zz = (z + NZ // 2 + i) % NZ

            for q in range(PARTS):
                for h in range(2):

                    @pl.when(jnp.logical_not(jnp.logical_and(self_feed, zz == z)))
                    def _():
                        sent(hv.at[pl.ds(q * T, T), pl.ds(COL * h, COL)], dsend.at[i, q * 2 + h])

            return carry

        lax.fori_loop(0, NZ, drain, 0)

    for cp in swaps:
        cp.wait_send()
    for d in range(1, NY):
        sent(mine, lsend.at[d])
        sent(gy.at[y], gysend.at[d])
    for d in range(1, NZ):
        sent(gz.at[z], gzsend.at[d])
    sent(pv.at[c], csend)

    def drain_chunk(k, carry):
        for d in range(1, NY):
            sent(sr.at[k, y], ssend.at[k, d])
            sent(ps.at[k, d - 1], psend.at[k, d])
            sent(hr.at[k, y], hsend.at[k, d])
        for j in range(NZ):

            @pl.when(j != z)
            def _():
                sent(zs.at[k, j], zsend.at[k, j])

        @pl.when(s < NS - 1)
        def _():
            for d in range(NZ):
                sent(yo.at[k], ysend.at[k, d])

        return carry

    lax.fori_loop(0, K, drain_chunk, 0)


def per_device(hidden_in, norm_gain, gate_weight, up_weight, down_weight, lengths):
    down = down_weight.reshape(4, 256, down_weight.shape[2])
    dma = pltpu.SemaphoreType.DMA
    any_space = pl.BlockSpec(memory_space=pl.ANY)
    return pl.pallas_call(
        kernel,
        out_shape=jax.ShapeDtypeStruct((1, SENT // NY, SENT), F32),
        in_specs=[any_space] * 5 + [pl.BlockSpec(memory_space=pltpu.SMEM)],
        out_specs=pl.BlockSpec(memory_space=pltpu.VMEM),
        scratch_shapes=[
            pltpu.VMEM((32, 256), BF16),
            pltpu.VMEM((1, ROWS), F32),
            pltpu.VMEM((NY, ROWS, SUB), BF16),
            pltpu.VMEM((NY, ROWS, SUB), BF16),
            pltpu.VMEM((2, 4, 256, 512), BF16),
            pltpu.VMEM((K, NZ, T, COL), BF16),
            pltpu.VMEM((K, NY - 1, T, 2 * SUB), BF16),
            pltpu.VMEM((K, NY, T, 2 * SUB), BF16),
            pltpu.VMEM((K, NY, 1, 128), F32),
            pltpu.VMEM((K, NY, T, SUB), BF16),
            pltpu.VMEM((K, NZ, T, COL), BF16),
            pltpu.VMEM((K, NZ, T, COL), BF16),
            pltpu.VMEM((K, T, COL), BF16),
            pltpu.VMEM((SENT, LEN, 128), F32),
            pltpu.VMEM((2, SENT // 2, COL), F32),
            pltpu.VMEM((NZ, SENT, 128), F32),
            pltpu.VMEM((NY, SENT, 128), F32),
            pltpu.VMEM((NY, SENT // NY, 128), F32),
            dma((2,)),
            dma((5,)),
            dma((3,)),
            dma((3,)),
            dma((NZ, 2 * PARTS)),
            dma((K, NZ)),
            dma((K, NY)),
            dma((K, NY)),
            dma((K, NY)),
            dma((K, NY)),
            dma((K, NY)),
            dma((K, NY)),
            dma((K, NZ)),
            dma((K, NZ)),
            dma((K, NZ)),
            dma((NY,)),
            dma((NY,)),
            dma,
            dma,
            dma((NZ,)),
            dma((NZ,)),
            dma((NY,)),
            dma((NY,)),
        ],
        compiler_params=pltpu.CompilerParams(
            collective_id=0, has_side_effects=True, vmem_limit_bytes=40 * 1024 * 1024
        ),
    )(hidden_in, norm_gain, gate_weight, up_weight, down, lengths)


def solution(mesh):
    placed = (
        P("dp", "tensor"),
        P("section", None),
        P("section", "dp", "tensor"),
        P("section", "dp", "tensor"),
        P("section", "dp", "tensor"),
        P("dp"),
    )
    return jax.shard_map(
        per_device, mesh=mesh, in_specs=placed, out_specs=P("section", "dp", None), check_vma=False
    )
```

time: 380 us -> 102 us (0.27)
  waiting for transfers between devices: 230 us -> 0 us
  Pallas kernels: 0 us -> 95.5 us
  starting transfers between devices: 56.6 us -> 0 us
  matrix products: 41.6 us -> 0 us
  between operations: 13.5 us -> 0.02 us
  local copies, waits for them, and re-layouts: 17.8 us -> 6.34 us
  other arithmetic: 8.68 us -> 0 us
  blocking collectives: 8.34 us -> 0 us
    all_gather x1 -> x0, waiting for transfers between devices: 102 us -> none  [side_by_side(): lax.all_gather(both, axis, axis=dim, tiled=True)]
    all_to_all x11 -> x0, waiting for transfers between devices: 99.2 us -> none  [the longest x6 53.5 us: sent_to_all(): return lax.all_to_all(copies, axis, split_axis=0, concat_axis=0, tiled=True)]
    pallas_call x0 -> x1, Pallas kernels: none -> 95.5 us  [per_device(): pl.pallas_call(kernel, out_shape=jax.ShapeDtypeStruct((1, SENT // NY, SEN...]
    all_to_all x11 -> x0, starting transfers between devices: 50.1 us -> none  [the longest x6 26.2 us: sent_to_all(): return lax.all_to_all(copies, axis, split_axis=0, concat_axis=0, tiled=True)]
    dot_general x11 -> x0, matrix products: 41.6 us -> none  [the longest x5 26.4 us: advance(): lax.dot_general(hidden, down_full, CONTRACT_LAST, preferred_element_type=...]
    ppermute x5 -> x0, waiting for transfers between devices: 28.3 us -> none  [passed_along(): return lax.ppermute(array, axis, pairs)]
    split x1 -> x0, local copies, waits for them, and re-layouts: 9.23 us -> none  [side_by_side(): jnp.split(lax.all_gather(both, axis, axis=dim, tiled=True), ends, axis=al...]
    all_to_all x1 -> x0, blocking collectives: 8.34 us -> none  [sent_to_all(): return lax.all_to_all(copies, axis, split_axis=0, concat_axis=0, tiled=True)]
  transfers between devices with their start and end apart: 17 -> 0, of which waited for: 17 -> 0; matrix products, arithmetic and copies ran while one was open for 1% -> 0% of each run, Pallas kernels for 0% -> 0%
where the time goes in v1:
time: 102 us
  Pallas kernels  95.5 us (94%)
  local copies, waits for them, and re-layouts  6.34 us (6%)
    pallas_call x1, Pallas kernels, per_device(): pl.pallas_call(kernel, out_shape=jax.ShapeDtypeStruct((1, SENT // NY, SEN...  95.5 us
    unnamed x13, local copies, waits for them, and re-layouts  6.34 us

profile of v1, /device:TPU:7, one launch (start us, length us, event | category | flops | bytes accessed | tf_op | source)
XLA Modules:
  0.0 101.8 jit_solution(2591017332196075238)
XLA Ops:
  0.0 0.0 copy-start.5
  0.0 0.7 copy-done.5
  0.7 0.0 copy-start
  0.7 1.2 %copy-done = bf16[1,1024,512]{2,1,0:T(8,128)(2,1)S(1)} copy-done((bf16[1,1024,512]{2,1,0:T(8,128)(2,1)S(1)}, bf16[1,1024,512]{2,1,0:T(8,128)(2,1)}, u32[]{:S(2)}) %copy-start) | copy-done | bytes 1048600
  1.9 0.0 copy-start.1
  1.9 1.2 %copy-done.1 = bf16[1,1024,512]{2,1,0:T(8,128)(2,1)S(1)} copy-done((bf16[1,1024,512]{2,1,0:T(8,128)(2,1)S(1)}, bf16[1,1024,512]{2,1,0:T(8,128)(2,1)}, u32[]{:S(2)}) %copy-start.1) | copy-done | bytes 1048600
  3.1 0.0 copy-start.2
  3.1 1.2 %copy-done.2 = bf16[1,1024,512]{2,1,0:T(8,128)(2,1)S(1)} copy-done((bf16[1,1024,512]{2,1,0:T(8,128)(2,1)S(1)}, bf16[1,1024,512]{2,1,0:T(8,128)(2,1)}, u32[]{:S(2)}) %copy-start.2) | copy-done | bytes 1048600
  4.3 0.0 copy-start.3
  4.3 0.7 copy-done.3
  5.0 0.0 copy-start.4
  5.1 0.7 copy-done.4
  5.8 95.5 %shard_map.64 = f32[1,4,16]{2,1,0:T(4,128)S(1)} custom-call(bf16[32,256]{1,0:T(8,128)(2,1)S(1)} %copy-done.3, f32[1,4096]{1,0:T(1,128)S(1)} %copy-done.4, bf16[1,1024,512]{2,1,0:T(8,128)(2,1)S(1)} %copy-done, bf16[1,1024,512]{2,1,0:T(8,128)(2,1)S(1)} %copy-done.1, bf16[4,256,512]{2,1,0:T(8,128)(2,1)S(1)} %bitcast.1, s32[4]{0:T(128)S(1)} %copy-done.5), custom_call_target="tpu_custom_call" | custom-call | tf_op jit(solution)/shard_map/pallas_call | solution.py:367
  101.3 0.6 copy.8
Async XLA Ops:
  0.0 0.7 copy-start.5
  0.7 1.2 %copy-start = (bf16[1,1024,512]{2,1,0:T(8,128)(2,1)S(1)}, bf16[1,1024,512]{2,1,0:T(8,128)(2,1)}, u32[]{:S(2)}) copy-start(bf16[1,1024,512]{2,1,0:T(8,128)(2,1)} %gate_in.1) | copy-start | bytes 3145732
  1.9 1.2 %copy-start.1 = (bf16[1,1024,512]{2,1,0:T(8,128)(2,1)S(1)}, bf16[1,1024,512]{2,1,0:T(8,128)(2,1)}, u32[]{:S(2)}) copy-start(bf16[1,1024,512]{2,1,0:T(8,128)(2,1)} %up_in.1) | copy-start | bytes 3145732
  3.1 1.2 %copy-start.2 = (bf16[1,1024,512]{2,1,0:T(8,128)(2,1)S(1)}, bf16[1,1024,512]{2,1,0:T(8,128)(2,1)}, u32[]{:S(2)}) copy-start(bf16[1,1024,512]{2,1,0:T(8,128)(2,1)} %param.10) | copy-start | bytes 3145732
  4.3 0.7 copy-start.3
  5.0 0.7 copy-start.4
